TPU v7x, 16 devices: a whole 2x2x2 slice. The times are simulated.
16 devices in a mesh: data: 4 (over z, y), tp: 4 (over x, core).
Axes of the slice: x: 2, y: 2, z: 2, core: 2. Of those that a mesh axis runs over, the one named last changes fastest.
Arguments:
- x_one: bfloat16 [1024, 49152], P('data', 'tp'), parts along dimension 0
- x_two: bfloat16 [1024, 49152], P('data', 'tp'), parts along dimension 0
- w_down: bfloat16 [49152, 12288], P('tp')
Outputs:
- output 1: bfloat16 [1024, 12288], P('data'), parts along dimension 0
- output 2: bfloat16 [1024, 12288], P('data'), parts along dimension 0
There are 4 independent parts. A program takes and returns all parts, laid end to end along the dimension named above; an argument that names none is the same for every part.
All inputs are finite; a program needn't handle non-finite values.
Results may differ from a plain program's by a relative error of at most 0.010606.
Values are sent between devices in bfloat16 or wider.
A program may use at most 1.25 GiB of HBM per device.

v0:
```python
import jax
import jax.numpy as jnp
from jax import lax
from jax.sharding import PartitionSpec as P


def solution(mesh):
    def per_device(x_one, x_two, w_down):
        part_one = jnp.dot(x_one, w_down, preferred_element_type=jnp.float32).astype(jnp.bfloat16)
        part_two = jnp.dot(x_two, w_down, preferred_element_type=jnp.float32).astype(jnp.bfloat16)
        y_one = lax.psum(part_one, "tp")
        y_two = lax.psum(part_two, "tp")
        return y_one, y_two

    return jax.shard_map(
        per_device,
        mesh=mesh,
        in_specs=(P("data", "tp"), P("data", "tp"), P("tp", None)),
        out_specs=(P("data", None), P("data", None)),
        check_vma=False,
    )
```

profile of v0, /device:TPU:0, one launch (start us, length us, event | category | flops | bytes accessed | tf_op | source)
XLA Modules:
  0.0 459.7 jit_solution(16191258770333810460)
XLA Ops:
  7.2 0.0 all-reduce.3.cloned.1.call-start
  7.2 108.5 %convolution_convert_fusion.1 = bf16[256,12288]{1,0:T(8,128)(2,1)} fusion(bf16[256,12288]{1,0:T(8,128)(2,1)} %param.3, bf16[12288,12288]{1,0:T(8,128)(2,1)} %param.5), kind=kOutput, calls=%fused_computation.1 | convolution fusion | flops 77312557056 | bytes 314572800 | tf_op jit(solution)/shard_map/dot_general | solution.py:9
  115.7 108.4 %convolution_convert_fusion = bf16[256,12288]{1,0:T(8,128)(2,1)} fusion(bf16[256,12288]{1,0:T(8,128)(2,1)} %param.4, bf16[12288,12288]{1,0:T(8,128)(2,1)} %param.5), kind=kOutput, calls=%fused_computation | convolution fusion | flops 77312557056 | bytes 314572800 | tf_op jit(solution)/shard_map/dot_general | solution.py:10
  224.1 0.0 all-reduce.3.cloned.1.call-update
  224.1 219.7 %all-reduce.3.cloned.1.call-done = (bf16[256,12288]{1,0:T(8,128)(2,1)}, bf16[256,12288]{1,0:T(8,128)(2,1)}) async-done(((bf16[256,12288]{1,0:T(8,128)(2,1)}, bf16[256,12288]{1,0:T(8,128)(2,1)}), (bf16[256,12288]{1,0:T(8,128)(2,1)}, bf16[256,12288]{1,0:T(8,128)(2,1)})) %all-reduce.3.cloned.1.call-update) | async-done | bytes 12582928 | tf_op jit(solution)/shard_map/psum | solution.py:11
  443.8 0.0 copy-start
  443.8 6.3 %copy.7 = bf16[256,12288]{1,0:T(8,128)(2,1)} copy(bf16[256,12288]{1,0:T(8,128)(2,1)} %get-tuple-element.4) | data formatting | bytes 12582912
  450.1 0.0 copy-done
  450.1 2.7 copy.8
Async XLA Ops:
  7.2 436.7 %all-reduce.3.cloned.1.call-start = ((), (), s32[]{:S(2)}) async-start(), calls=%async_computation | async-start | bytes 25165824 | tf_op jit(solution)/shard_map/psum | solution.py:11
  443.8 6.3 %copy-start = (bf16[256,12288]{1,0:T(8,128)(2,1)S(1)}, bf16[256,12288]{1,0:T(8,128)(2,1)}, u32[]{:S(2)}) copy-start(bf16[256,12288]{1,0:T(8,128)(2,1)} %get-tuple-element.5) | copy-start | bytes 18874372
Sparse Core Ops, SparseCore 0:
  224.2 219.5 all-reduce.2
where the time goes:
time: 461 us; the launch traced here: 460 us
  waiting for transfers between devices  220 us (48%)
  matrix products  217 us (47%)
  between operations  14 us (3%)
  local copies, waits for them, and re-layouts  9 us (2%)
    psum x1, waiting for transfers between devices, per_device(): y_one = lax.psum(part_one, 'tp')  220 us
    dot_general x1, matrix products, per_device(): jnp.dot(x_one, w_down, preferred_element_type=jnp.float32)  108 us
    dot_general x1, matrix products, per_device(): jnp.dot(x_two, w_down, preferred_element_type=jnp.float32)  108 us
  transfers between devices with their start and end apart: 1, of which 1 were waited for; matrix products, arithmetic and copies ran while one was open for 0% of the time, Pallas kernels for 0%

commit v1 on v0

v1 whole, which is shorter than its diff:
```python
import jax
import jax.numpy as jnp
from jax import lax
from jax.experimental import pallas as pl
from jax.experimental.pallas import tpu as pltpu
from jax.sharding import PartitionSpec as P

MESH = pl.DeviceIdType.MESH
BF16 = jnp.bfloat16
F32 = jnp.float32

COLS = 512
PIECES = 6


def mod(j, n):
    return j % n if isinstance(j, int) else lax.rem(j, n)


def kernel(x1, x2, w, y1, y2, X, W, Ps, R, own, A, B, Y,
           xsem, w0sem, wsem, p_send, p_recv, a_send, a_recv, y_loc, y_send, y_recv):
    mb, depth = x1.shape
    width = w.shape[1]
    half = mb // 2
    n = width // COLS
    kp = depth // PIECES

    me = lax.axis_index("tp")
    core = lax.rem(me, 2)
    sib = me + 1 - 2 * core
    peer = lax.rem(me + 2, 4)
    r_own = pl.multiple_of(core * half, half)
    r_oth = pl.multiple_of((1 - core) * half, half)

    def col(j):
        return pl.ds(j * COLS if isinstance(j, int) else pl.multiple_of(j * COLS, COLS), COLS)

    def x_copies(i):
        ks = pl.ds(i * kp if isinstance(i, int) else pl.multiple_of(i * kp, kp), kp)
        return [
            pltpu.make_async_copy(src.at[pl.ds(row, half), ks], X.at[pl.ds(g * half, half), ks], xsem.at[i, g])
            for g, (src, row) in enumerate(((x1, r_oth), (x2, r_oth), (x1, r_own), (x2, r_own)))
        ]

    def w0_copy(i):
        ks = pl.ds(i * kp if isinstance(i, int) else pl.multiple_of(i * kp, kp), kp)
        return pltpu.make_async_copy(w.at[ks, col(0)], W.at[0, ks], w0sem.at[i])

    def w_copies(j):
        s = mod(j, 3)
        kh = depth // 2
        return [
            pltpu.make_async_copy(w.at[pl.ds(i * kh, kh), col(j)], W.at[s, pl.ds(i * kh, kh)], wsem.at[s, i])
            for i in range(2)
        ]

    def p_copy(j):
        s = mod(j, 2)
        return pltpu.make_async_remote_copy(
            src_ref=Ps.at[s], dst_ref=R.at[s], send_sem=p_send.at[s], recv_sem=p_recv.at[s],
            device_id={"tp": sib}, device_id_type=MESH)

    def a_copy(j):
        s, t = mod(j, 4), mod(j, 5)
        return pltpu.make_async_remote_copy(
            src_ref=A.at[s], dst_ref=B.at[t], send_sem=a_send.at[s], recv_sem=a_recv.at[t],
            device_id={"tp": peer}, device_id_type=MESH)

    def y_copies(j):
        s, t = mod(j, 2), mod(j, 4)
        out = []
        for g, y in enumerate((y1, y2)):
            src = Y.at[s, pl.ds(g * half, half)]
            dst = y.at[pl.ds(r_own, half), col(j)]
            out.append(pltpu.make_async_copy(src, dst, y_loc.at[s, g]))
            out.append(pltpu.make_async_remote_copy(
                src_ref=src, dst_ref=dst, send_sem=y_send.at[s, g], recv_sem=y_recv.at[t, g],
                device_id={"tp": sib}, device_id_type=MESH))
        return out

    def start(copies):
        for c in copies:
            c.start()

    def wait(copies):
        for c in copies:
            c.wait()

    def pair_sum(j):
        A[mod(j, 4)] = (own[...] + R[mod(j, 2)]).astype(BF16)

    def total(j, a, b):
        Y[mod(j, 2)] = (A[a].astype(F32) + B[b].astype(F32)).astype(BF16)

    def mul_oth(j):
        Ps[mod(j, 2)] = jnp.dot(X[pl.ds(0, mb), :], W[mod(j, 3)], preferred_element_type=F32)

    def mul_own(j):
        own[...] = jnp.dot(X[pl.ds(mb, mb), :], W[mod(j, 3)], preferred_element_type=F32)

    for i in range(PIECES):
        start(x_copies(i))
        w0_copy(i).start()
    for j in (1, 2):
        start(w_copies(j))

    barrier = pltpu.get_barrier_semaphore()
    for other in (sib, peer):
        pl.semaphore_signal(barrier, inc=1, device_id={"tp": other}, device_id_type=MESH)
    pl.semaphore_wait(barrier, 2)

    Ps[0] = jnp.zeros((mb, COLS), F32)
    own[...] = jnp.zeros((mb, COLS), F32)

    def first(i, carry):
        w0_copy(i).wait()
        wait(x_copies(i))
        ks = pl.ds(pl.multiple_of(i * kp, kp), kp)
        d = jnp.dot(X[:, ks], W[0, ks, :], preferred_element_type=F32)
        Ps[0] += d[:mb]
        own[...] += d[mb:]
        return carry

    lax.fori_loop(0, PIECES, first, 0)
    p_copy(0).start()
    wait(w_copies(1))
    mul_oth(1)

    def bound(j, guard):
        wait(w_copies(j + 1))
        p_copy(j - 1).wait()
        pair_sum(j - 1)
        p_copy(j).start()
        start(w_copies(j + 2))
        guard(j >= 3, lambda: a_copy(j - 3).wait())
        guard(j >= 5, lambda: wait(y_copies(j - 5)))
        a_copy(j - 1).start()
        guard(j >= 4, lambda: start(y_copies(j - 4)))

    def step(j, carry):
        bound(j, lambda c, f: pl.when(c)(f))
        total(j + 1, mod(j + 1, 4), mod(j + 2, 5))
        mul_oth(j + 1)
        mul_own(j)
        return carry

    m = n - 3
    lax.fori_loop(1, m, step, 0)

    def tot(j):
        total(j, j % 4, j % 5)

    bound(m, lambda c, f: f())
    tot(m - 3)
    mul_own(m)

    p_copy(m).wait()
    pair_sum(m)
    a_copy(m - 2).wait()
    wait(y_copies(m - 4))
    a_copy(m).start()
    start(y_copies(m - 3))
    tot(m - 2)
    mul_oth(m + 1)

    p_copy(m + 1).start()
    start(y_copies(m - 2))
    wait(w_copies(m + 2))
    wait(y_copies(m - 3))
    mul_own(m + 1)

    p_copy(m + 1).wait()
    pair_sum(m + 1)
    a_copy(m - 1).wait()
    a_copy(m + 1).start()
    tot(m - 1)
    mul_oth(m + 2)

    wait(y_copies(m - 2))
    p_copy(m + 2).start()
    start(y_copies(m - 1))
    a_copy(m).wait()
    tot(m)
    mul_own(m + 2)

    p_copy(m + 2).wait()
    pair_sum(m + 2)
    wait(y_copies(m - 1))
    start(y_copies(m))
    a_copy(m + 2).start()
    a_copy(m + 1).wait()
    tot(m + 1)
    wait(y_copies(m))
    start(y_copies(m + 1))
    a_copy(m + 2).wait()
    tot(m + 2)
    start(y_copies(m + 2))
    wait(y_copies(m + 1))
    wait(y_copies(m + 2))


def solution(mesh):
    def per_device(x_one, x_two, w_down):
        mb, depth = x_one.shape
        width = w_down.shape[1]
        hbm = pl.BlockSpec(memory_space=pltpu.HBM)
        dma = pltpu.SemaphoreType.DMA
        return pl.pallas_call(
            kernel,
            out_shape=[jax.ShapeDtypeStruct((mb, width), BF16)] * 2,
            in_specs=[hbm] * 3,
            out_specs=[hbm] * 2,
            scratch_shapes=[
                pltpu.VMEM((2 * mb, depth), BF16),
                pltpu.VMEM((3, depth, COLS), BF16),
                pltpu.VMEM((2, mb, COLS), F32),
                pltpu.VMEM((2, mb, COLS), F32),
                pltpu.VMEM((mb, COLS), F32),
                pltpu.VMEM((4, mb, COLS), BF16),
                pltpu.VMEM((5, mb, COLS), BF16),
                pltpu.VMEM((2, mb, COLS), BF16),
                dma((PIECES, 4)), dma((PIECES,)), dma((3, 2)),
                dma((2,)), dma((2,)), dma((4,)), dma((5,)),
                dma((2, 2)), dma((2, 2)), dma((4, 2)),
            ],
            compiler_params=pltpu.CompilerParams(
                collective_id=0, has_side_effects=True, vmem_limit_bytes=60 * 1024 * 1024),
        )(x_one, x_two, w_down)

    return jax.shard_map(
        per_device,
        mesh=mesh,
        in_specs=(P("data", "tp"), P("data", "tp"), P("tp", None)),
        out_specs=(P("data", None), P("data", None)),
        check_vma=False,
    )
```

time: 461 us -> 194 us (0.42)
  waiting for transfers between devices: 220 us -> 0 us
  matrix products: 217 us -> 0 us
  Pallas kernels: 0 us -> 184 us
  between operations: 14 us -> 0.65 us
    psum x1 -> x0, waiting for transfers between devices: 220 us -> none  [per_device(): y_one = lax.psum(part_one, 'tp')]
    dot_general x2 -> x0, matrix products: 217 us -> none  [the longest x1 108 us: per_device(): jnp.dot(x_one, w_down, preferred_element_type=jnp.float32)]
    pallas_call x0 -> x1, Pallas kernels: none -> 184 us  [per_device(): pl.pallas_call(kernel, out_shape=[jax.ShapeDtypeStruct((mb, width), BF16)...]
  transfers between devices with their start and end apart: 1 -> 0, of which waited for: 1 -> 0; matrix products, arithmetic and copies ran while one was open for 0% -> 0% of each run, Pallas kernels for 0% -> 0%
where the time goes in v1:
time: 194 us
  Pallas kernels  184 us (95%)
  local copies, waits for them, and re-layouts  9 us (5%)
    pallas_call x1, Pallas kernels, per_device(): pl.pallas_call(kernel, out_shape=[jax.ShapeDtypeStruct((mb, width), BF16)...  184 us
    unnamed x4, local copies, waits for them, and re-layouts  9 us

profile of v1, /device:TPU:0, one launch (start us, length us, event | category | flops | bytes accessed | tf_op | source)
XLA Modules:
  0.0 193.6 jit_solution(16228948551895049413)
XLA Ops:
  0.6 183.9 %shard_map.50 = (bf16[256,12288]{1,0:T(8,128)(2,1)}, bf16[256,12288]{1,0:T(8,128)(2,1)}) custom-call(bf16[256,12288]{1,0:T(8,128)(2,1)} %x1.1, bf16[256,12288]{1,0:T(8,128)(2,1)} %x2.1, bf16[12288,12288]{1,0:T(8,128)(2,1)} %w.1), custom_call_target="tpu_custom_call" | custom-call | tf_op jit(solution)/shard_map/pallas_call | solution.py:208
  184.6 0.0 copy-start
  184.6 6.3 %copy.7 = bf16[256,12288]{1,0:T(8,128)(2,1)} copy(bf16[256,12288]{1,0:T(8,128)(2,1)} %get-tuple-element.4) | data formatting | bytes 12582912
  190.9 0.0 copy-done
  190.9 2.7 %copy.8 = bf16[256,12288]{1,0:T(8,128)(2,1)} copy(bf16[256,12288]{1,0:T(8,128)(2,1)S(1)} %copy-done) | data formatting | bytes 12582912
Async XLA Ops:
  184.6 6.3 %copy-start = (bf16[256,12288]{1,0:T(8,128)(2,1)S(1)}, bf16[256,12288]{1,0:T(8,128)(2,1)}, u32[]{:S(2)}) copy-start(bf16[256,12288]{1,0:T(8,128)(2,1)} %get-tuple-element.5) | copy-start | bytes 18874372

commit v2 on v1

v2 whole, which is shorter than its diff:
```python
import jax
import jax.numpy as jnp
from jax import lax
from jax.experimental import pallas as pl
from jax.experimental.pallas import tpu as pltpu
from jax.sharding import PartitionSpec as P

MESH = pl.DeviceIdType.MESH
BF16 = jnp.bfloat16
F32 = jnp.float32

COLS = 512
PIECES = 6


def mod(j, n):
    return j % n if isinstance(j, int) else lax.rem(j, n)


def kernel(x1, x2, w, y1, y2, X, W, Ps, R, own, A, B,
           xsem, w0sem, wsem, p_send, p_recv, a_send, a_recv, y_send, y_recv):
    mb, depth = x1.shape
    width = w.shape[1]
    half = mb // 2
    n = width // COLS
    kp = depth // PIECES

    me = lax.axis_index("tp")
    core = lax.rem(me, 2)
    sib = me + 1 - 2 * core
    peer = lax.rem(me + 2, 4)
    r_own = pl.multiple_of(core * half, half)
    r_oth = pl.multiple_of((1 - core) * half, half)

    def col(j):
        return pl.ds(j * COLS if isinstance(j, int) else pl.multiple_of(j * COLS, COLS), COLS)

    def x_copies(i):
        ks = pl.ds(i * kp if isinstance(i, int) else pl.multiple_of(i * kp, kp), kp)
        return [
            pltpu.make_async_copy(src.at[pl.ds(row, half), ks], X.at[pl.ds(g * half, half), ks], xsem.at[i, g])
            for g, (src, row) in enumerate(((x1, r_oth), (x2, r_oth), (x1, r_own), (x2, r_own)))
        ]

    def w0_copy(i):
        ks = pl.ds(i * kp if isinstance(i, int) else pl.multiple_of(i * kp, kp), kp)
        return pltpu.make_async_copy(w.at[ks, col(0)], W.at[0, ks], w0sem.at[i])

    def w_copies(j):
        s = mod(j, 2)
        kh = depth // 2
        return [
            pltpu.make_async_copy(w.at[pl.ds(i * kh, kh), col(j)], W.at[s, pl.ds(i * kh, kh)], wsem.at[s, i])
            for i in range(2)
        ]

    def p_copy(j):
        s = mod(j, 2)
        return pltpu.make_async_remote_copy(
            src_ref=Ps.at[s], dst_ref=R.at[s], send_sem=p_send.at[s], recv_sem=p_recv.at[s],
            device_id={"tp": sib}, device_id_type=MESH)

    def a_copy(j):
        s, t = mod(j, 4), mod(j, 8)
        return pltpu.make_async_remote_copy(
            src_ref=A.at[s], dst_ref=B.at[t], send_sem=a_send.at[s], recv_sem=a_recv.at[t],
            device_id={"tp": peer}, device_id_type=MESH)

    def y_copies(j):
        s, t = mod(j, 2), mod(j, 4)
        out = []
        for g, y in enumerate((y1, y2)):
            ref = y.at[pl.ds(r_own, half), col(j)]
            out.append(pltpu.make_async_remote_copy(
                src_ref=ref, dst_ref=ref, send_sem=y_send.at[s, g], recv_sem=y_recv.at[t, g],
                device_id={"tp": sib}, device_id_type=MESH))
        return out

    def start(copies):
        for c in copies:
            c.start()

    def wait(copies):
        for c in copies:
            c.wait()

    def pair_sum(j):
        A[mod(j, 4)] = (own[mod(j, 2)] + R[mod(j, 2)]).astype(BF16)

    def total(j, c=None):
        v = (A[mod(j, 4)].astype(F32) + B[mod(j, 8)].astype(F32)).astype(BF16)
        for g, y in enumerate((y1, y2)):
            y[pl.ds(r_own, half), col(j if c is None else c)] = v[g * half : (g + 1) * half]

    def mul(j):
        s = mod(j, 2)
        d = jnp.dot(X[...], W[s], preferred_element_type=F32)
        Ps[s] = d[:mb]
        own[s] = d[mb:]

    def mul_oth(j):
        Ps[j % 2] = jnp.dot(X[pl.ds(0, mb), :], W[j % 2], preferred_element_type=F32)

    def mul_own(j):
        own[j % 2] = jnp.dot(X[pl.ds(mb, mb), :], W[j % 2], preferred_element_type=F32)

    for i in range(PIECES):
        start(x_copies(i))
        w0_copy(i).start()
    start(w_copies(1))

    barrier = pltpu.get_barrier_semaphore()
    for other in (sib, peer):
        pl.semaphore_signal(barrier, inc=1, device_id={"tp": other}, device_id_type=MESH)
    pl.semaphore_wait(barrier, 2)

    Ps[0] = jnp.zeros((mb, COLS), F32)
    own[0] = jnp.zeros((mb, COLS), F32)

    def first(i, carry):
        w0_copy(i).wait()
        wait(x_copies(i))
        ks = pl.ds(pl.multiple_of(i * kp, kp), kp)
        d = jnp.dot(X[:, ks], W[0, ks, :], preferred_element_type=F32)
        Ps[0] += d[:mb]
        own[0] += d[mb:]
        return carry

    lax.fori_loop(0, PIECES, first, 0)

    def bound(j, guard):
        wait(w_copies(j))

        guard(j >= 2, lambda: p_copy(j - 2).wait())
        pair_sum(j - 2 if isinstance(j, int) else j + 2)
        p_copy(j - 1).start()
        start(w_copies(j + 1))
        guard(j >= 4, lambda: a_copy(j - 4).wait())
        guard(j >= 6, lambda: wait(y_copies(j - 6)))
        guard(j >= 2, lambda: a_copy(j - 2).start())
        guard(j >= 5, lambda: start(y_copies(j - 5)))

    def step(j, carry):
        bound(j, lambda c, f: pl.when(c)(f))
        total(j + 4, lax.max(j - 4, 0))
        mul(j)
        return carry

    m = n - 3
    lax.fori_loop(1, m, step, 0)

    bound(m, lambda c, f: f())
    total(m - 4)
    mul_oth(m)

    p_copy(m - 1).wait()
    pair_sum(m - 1)
    p_copy(m).start()
    a_copy(m - 3).wait()
    wait(y_copies(m - 5))
    a_copy(m - 1).start()
    start(y_copies(m - 4))
    total(m - 3)
    mul_own(m)

    p_copy(m).wait()
    pair_sum(m)
    start(y_copies(m - 3))
    wait(w_copies(m + 1))
    start(w_copies(m + 2))
    a_copy(m).start()
    mul_oth(m + 1)

    a_copy(m - 2).wait()
    wait(y_copies(m - 4))
    p_copy(m + 1).start()
    total(m - 2)
    mul_own(m + 1)

    p_copy(m + 1).wait()
    pair_sum(m + 1)
    a_copy(m - 1).wait()
    wait(y_copies(m - 3))
    start(y_copies(m - 2))
    wait(w_copies(m + 2))
    a_copy(m + 1).start()
    total(m - 1)
    mul_oth(m + 2)

    wait(y_copies(m - 2))
    p_copy(m + 2).start()
    start(y_copies(m - 1))
    mul_own(m + 2)

    p_copy(m + 2).wait()
    pair_sum(m + 2)
    wait(y_copies(m - 1))
    a_copy(m).wait()
    a_copy(m + 2).start()
    total(m)
    start(y_copies(m))
    a_copy(m + 1).wait()
    total(m + 1)
    wait(y_copies(m))
    start(y_copies(m + 1))
    a_copy(m + 2).wait()
    total(m + 2)
    start(y_copies(m + 2))
    wait(y_copies(m + 1))
    wait(y_copies(m + 2))


def solution(mesh):
    def per_device(x_one, x_two, w_down):
        mb, depth = x_one.shape
        width = w_down.shape[1]
        hbm = pl.BlockSpec(memory_space=pltpu.HBM)
        dma = pltpu.SemaphoreType.DMA
        return pl.pallas_call(
            kernel,
            out_shape=[pltpu.VMEM((mb, width), BF16)] * 2,
            in_specs=[hbm] * 3,
            out_specs=[pl.BlockSpec(memory_space=pltpu.VMEM)] * 2,
            scratch_shapes=[
                pltpu.VMEM((2 * mb, depth), BF16),
                pltpu.VMEM((2, depth, COLS), BF16),
                pltpu.VMEM((2, mb, COLS), F32),
                pltpu.VMEM((2, mb, COLS), F32),
                pltpu.VMEM((2, mb, COLS), F32),
                pltpu.VMEM((4, mb, COLS), BF16),
                pltpu.VMEM((8, mb, COLS), BF16),
                dma((PIECES, 4)), dma((PIECES,)), dma((2, 2)),
                dma((2,)), dma((2,)), dma((4,)), dma((8,)),
                dma((2, 2)), dma((4, 2)),
            ],
            compiler_params=pltpu.CompilerParams(
                collective_id=0, has_side_effects=True, vmem_limit_bytes=50 * 1024 * 1024),
        )(x_one, x_two, w_down)

    return jax.shard_map(
        per_device,
        mesh=mesh,
        in_specs=(P("data", "tp"), P("data", "tp"), P("tp", None)),
        out_specs=(P("data", None), P("data", None)),
        check_vma=False,
    )
```

time: 194 us -> 188 us (0.969)
  local copies, waits for them, and re-layouts: 9 us -> 5.41 us
  Pallas kernels: 184 us -> 182 us
    unnamed x4 -> x2, local copies, waits for them, and re-layouts: 9 us -> 5.41 us
where the time goes in v2:
time: 188 us
  Pallas kernels  182 us (97%)
  local copies, waits for them, and re-layouts  5.41 us (3%)
    pallas_call x1, Pallas kernels, per_device(): pl.pallas_call(kernel, out_shape=[pltpu.VMEM((mb, width), BF16)] * 2, in_...  182 us
    unnamed x2, local copies, waits for them, and re-layouts  5.41 us

profile of v2, /device:TPU:0, one launch (start us, length us, event | category | flops | bytes accessed | tf_op | source)
XLA Modules:
  0.0 188.2 jit_solution(10757804267921005303)
XLA Ops:
  0.6 182.2 %shard_map.50 = (bf16[256,12288]{1,0:T(8,128)(2,1)S(1)}, bf16[256,12288]{1,0:T(8,128)(2,1)S(1)}) custom-call(bf16[256,12288]{1,0:T(8,128)(2,1)} %x1.1, bf16[256,12288]{1,0:T(8,128)(2,1)} %x2.1, bf16[12288,12288]{1,0:T(8,128)(2,1)} %w.1), custom_call_target="tpu_custom_call" | custom-call | tf_op jit(solution)/shard_map/pallas_call | solution.py:219
  182.8 2.7 %copy.7 = bf16[256,12288]{1,0:T(8,128)(2,1)} copy(bf16[256,12288]{1,0:T(8,128)(2,1)S(1)} %get-tuple-element.2) | data formatting | bytes 12582912
  185.5 2.7 %copy.8 = bf16[256,12288]{1,0:T(8,128)(2,1)} copy(bf16[256,12288]{1,0:T(8,128)(2,1)S(1)} %get-tuple-element.3) | data formatting | bytes 12582912

commit v3 on v2

--- a/solution.py
+++ b/solution.py
@@ -150,8 +150,8 @@
     lax.fori_loop(1, m, step, 0)
 
     bound(m, lambda c, f: f())
+    mul_oth(m)
     total(m - 4)
-    mul_oth(m)
 
     p_copy(m - 1).wait()
     pair_sum(m - 1)
@@ -160,8 +160,8 @@
     wait(y_copies(m - 5))
     a_copy(m - 1).start()
     start(y_copies(m - 4))
+    mul_own(m)
     total(m - 3)
-    mul_own(m)
 
     p_copy(m).wait()
     pair_sum(m)
@@ -174,8 +174,8 @@
     a_copy(m - 2).wait()
     wait(y_copies(m - 4))
     p_copy(m + 1).start()
+    mul_own(m + 1)
     total(m - 2)
-    mul_own(m + 1)
 
     p_copy(m + 1).wait()
     pair_sum(m + 1)
@@ -184,8 +184,8 @@
     start(y_copies(m - 2))
     wait(w_copies(m + 2))
     a_copy(m + 1).start()
+    mul_oth(m + 2)
     total(m - 1)
-    mul_oth(m + 2)
 
     wait(y_copies(m - 2))
     p_copy(m + 2).start()
@@ -210,13 +210,27 @@
     wait(y_copies(m + 2))
 
 
+def put_kernel(v1, v2, y1, y2, sem):
+    rows, width = v1.shape
+    part = width // 4
+    copies = [
+        pltpu.make_async_copy(v.at[:, pl.ds(i * part, part)], y.at[:, pl.ds(i * part, part)], sem.at[g, i])
+        for g, (v, y) in enumerate(((v1, y1), (v2, y2)))
+        for i in range(4)
+    ]
+    for c in copies:
+        c.start()
+    for c in copies:
+        c.wait()
+
+
 def solution(mesh):
     def per_device(x_one, x_two, w_down):
         mb, depth = x_one.shape
         width = w_down.shape[1]
         hbm = pl.BlockSpec(memory_space=pltpu.HBM)
         dma = pltpu.SemaphoreType.DMA
-        return pl.pallas_call(
+        totals = pl.pallas_call(
             kernel,
             out_shape=[pltpu.VMEM((mb, width), BF16)] * 2,
             in_specs=[hbm] * 3,
@@ -236,6 +250,14 @@
             compiler_params=pltpu.CompilerParams(
                 collective_id=0, has_side_effects=True, vmem_limit_bytes=50 * 1024 * 1024),
         )(x_one, x_two, w_down)
+        return pl.pallas_call(
+            put_kernel,
+            out_shape=[jax.ShapeDtypeStruct((mb, width), BF16)] * 2,
+            in_specs=[pl.BlockSpec(memory_space=pltpu.VMEM)] * 2,
+            out_specs=[hbm] * 2,
+            scratch_shapes=[dma((2, 4))],
+            compiler_params=pltpu.CompilerParams(vmem_limit_bytes=1024 * 1024),
+        )(*totals)
 
     return jax.shard_map(
         per_device,

time: 188 us -> 188 us (level)
  local copies, waits for them, and re-layouts: 5.41 us -> 0 us
  Pallas kernels: 182 us -> 187 us
    unnamed x2 -> x0, local copies, waits for them, and re-layouts: 5.41 us -> none
    pallas_call x0 -> x1, Pallas kernels: none -> 4.66 us  [per_device(): pl.pallas_call(put_kernel, out_shape=[jax.ShapeDtypeStruct((mb, width), B...]
where the time goes in v3:
time: 188 us
  Pallas kernels  187 us (99%)
    pallas_call x1, Pallas kernels, per_device(): pl.pallas_call(kernel, out_shape=[pltpu.VMEM((mb, width), BF16)] * 2, in_...  182 us
    pallas_call x1, Pallas kernels, per_device(): pl.pallas_call(put_kernel, out_shape=[jax.ShapeDtypeStruct((mb, width), B...  4.66 us

profile of v3, /device:TPU:0, one launch (start us, length us, event | category | flops | bytes accessed | tf_op | source)
XLA Modules:
  0.0 187.7 jit_solution(9725983262176075963)
XLA Ops:
  0.6 182.2 %shard_map.50 = (bf16[256,12288]{1,0:T(8,128)(2,1)S(1)}, bf16[256,12288]{1,0:T(8,128)(2,1)S(1)}) custom-call(bf16[256,12288]{1,0:T(8,128)(2,1)} %x1.1, bf16[256,12288]{1,0:T(8,128)(2,1)} %x2.1, bf16[12288,12288]{1,0:T(8,128)(2,1)} %w.1), custom_call_target="tpu_custom_call" | custom-call | tf_op jit(solution)/shard_map/pallas_call | solution.py:233
  182.8 4.7 %shard_map.51 = (bf16[256,12288]{1,0:T(8,128)(2,1)}, bf16[256,12288]{1,0:T(8,128)(2,1)}) custom-call(bf16[256,12288]{1,0:T(8,128)(2,1)S(1)} %get-tuple-element.4.v1, bf16[256,12288]{1,0:T(8,128)(2,1)S(1)} %get-tuple-element.5.v2), custom_call_target="tpu_custom_call" | custom-call | tf_op jit(solution)/shard_map/pallas_call | solution.py:253
